TPU v7x, 128 devices: a whole 4x4x4 slice. The times are simulated.
128 devices in a mesh: src: 16 (over z, x), rcv: 8 (over y, core).
Axes of the slice: x: 4, y: 4, z: 4, core: 2. Of those that a mesh axis runs over, the one named last changes fastest.
Arguments:
- traces: bfloat16 [2, 2, 2048, 2048], P(None, None, 'src', 'rcv'), may hold values from -8 to 8
- wavelet: float32 [2, 2], replicated, may hold values from -0.3 to 0.3
Outputs:
- coeffs: float32 [2, 2, 2048, 2048], P(None, None, 'src', 'rcv')
- norms: float32 [2, 2], replicated
All inputs are finite; a program needn't handle non-finite values.
Results may differ from a plain program's by a relative error of at most 0.006.
Values may be sent and summed in bfloat16 or wider, within the bound.
A program may use at most 128 MiB of HBM per device.

v0:
```python
import math
import jax
import jax.numpy as jnp
from jax import lax
from jax.sharding import Mesh
from jax.sharding import PartitionSpec as P

ITERS = 2
SRC = ("src_0", "src_1")
RCV = ("rcv_0", "rcv_1")
SRC_RCV = ("src_0", "src_1", "rcv_0", "rcv_1")
step_length = 0.4
shrink_fraction = 0.2


def laid_out(tiles, dim):
    shape = list(tiles.shape[1:])
    shape[dim] *= tiles.shape[0]
    return jnp.moveaxis(tiles, 0, dim).reshape(shape)


def copy_for_each(x, axis):
    copies = jnp.broadcast_to(x, (lax.axis_size(axis), *x.shape))
    return lax.all_to_all(copies, axis, split_axis=0, concat_axis=0, tiled=True)


def gathered_copies(x, axis, dim):
    return laid_out(copy_for_each(x, axis), dim)


def all_in_one(x, axis):
    leaves = jax.tree.leaves(x)
    order = sorted(range(len(leaves)), key=lambda k: -leaves[k].size)
    width = (1, *leaves[order[0]].shape)[-1]
    lines = [
        jnp.pad(leaves[k].reshape(-1), (0, -leaves[k].size % width)).reshape(-1, width)
        for k in order
    ]
    both, at, found = (lax.all_gather(jnp.concatenate(lines), axis), 0, {})
    for k, line in zip(order, lines):
        share = both[:, at : at + len(line)].reshape(len(both), -1)
        found[k] = share[:, : leaves[k].size].reshape(-1, *leaves[k].shape)
        at += len(line)
    numbers = iter(range(len(leaves)))
    return jax.tree.map(lambda _: found[next(numbers)], x)


def once_a_type(x, axis):
    leaves, found = (jax.tree.leaves(x), {})
    for first, a in enumerate(leaves):
        if first not in found:
            alike = [k for k, b in enumerate(leaves) if b.dtype == a.dtype]
            got = (
                all_in_one([leaves[k] for k in alike], axis)
                if len(alike) > 1
                else [lax.all_gather(a, axis)]
            )
            for k, b in zip(alike, got):
                found[k] = b
    numbers = iter(range(len(leaves)))
    return jax.tree.map(lambda _: found[next(numbers)], x)


def joined_all(x, axes, combine):
    for axis in axes:
        pieces = once_a_type(x, axis)
        x = jax.tree.map(lambda part: part[0], pieces)
        for k in range(1, lax.axis_size(axis)):
            x = combine(x, jax.tree.map(lambda part: part[k], pieces))
    return x


def table_block(offset, height, second, breadth, length, direction):
    left_index = offset + jnp.arange(height, dtype=jnp.int32)
    right_index = second + jnp.arange(breadth, dtype=jnp.int32)
    phase = left_index[:, None] * right_index[None, :] % length
    angle = phase.astype(jnp.float32) * (2.0 * math.pi / length)
    scale = 1.0 / math.sqrt(length)
    return jnp.stack([jnp.cos(angle) * scale, direction * (jnp.sin(angle) * scale)]).astype(
        jnp.bfloat16
    )


def complex_product(left_side, right_side, pattern, left_table, right_table):
    left_re = left_side[0] if left_table else left_side[:, 0]
    left_im = left_side[1] if left_table else left_side[:, 1]
    right_re = right_side[0] if right_table else right_side[:, 0]
    right_im = right_side[1] if right_table else right_side[:, 1]

    def single(first_op, second_op):
        return jnp.einsum(pattern, first_op, second_op, preferred_element_type=jnp.float32)

    real_part = single(left_re, right_re) - single(left_im, right_im)
    imag_part = single(left_re, right_im) + single(left_im, right_re)
    return jnp.stack([real_part, imag_part], axis=1)


def complex_scale(real_part, imag_part, values):
    return jnp.stack(
        [
            real_part * values[:, 0] - imag_part * values[:, 1],
            real_part * values[:, 1] + imag_part * values[:, 0],
        ],
        axis=1,
    )


def combine_stats(first_pair, second_pair):
    return (jnp.maximum(first_pair[0], second_pair[0]), first_pair[1] + second_pair[1])


def per_device(traces, wavelet):
    row_count = traces.shape[2]
    col_count = traces.shape[3]
    extent = row_count * lax.axis_size(SRC)
    row_anchor = lax.axis_index(SRC) * row_count
    col_anchor = lax.axis_index(RCV) * col_count
    root_scale = 1.0 / math.sqrt(extent)
    wave_re = (wavelet[:, 0] * root_scale)[:, None, None]
    wave_im = (wavelet[:, 1] * root_scale)[:, None, None]
    forward_cols = table_block(0, extent, col_anchor, col_count, extent, -1.0)
    forward_rows = table_block(row_anchor, row_count, 0, extent, extent, -1.0)
    inverse_cols = table_block(0, extent, col_anchor, col_count, extent, 1.0)
    inverse_rows = table_block(row_anchor, row_count, 0, extent, extent, 1.0)
    coeffs = jnp.zeros(traces.shape, jnp.float32)
    columns_all = lax.all_gather(traces, SRC, axis=2, tiled=True)
    traces_f = traces.astype(jnp.float32)

    def column_section(table, portion):
        return complex_product(table, portion, "mn,fnc->fmc", True, False)

    def paired(first_op, second_op):
        return jnp.einsum("fmr,fkr->fmk", first_op, second_op, preferred_element_type=jnp.float32)

    norm_list = []
    for iteration in range(ITERS):
        if iteration == 0:
            misfit = traces_f
        else:
            coeff_half = coeffs.astype(jnp.bfloat16)
            halfway = column_section(
                inverse_rows, lax.all_gather(coeff_half, SRC, axis=2, tiled=True)
            ).astype(jnp.bfloat16)
            model = complex_product(
                gathered_copies(halfway, RCV, 3), inverse_cols, "fmn,nc->fmc", False, True
            ).astype(jnp.bfloat16)
            product = complex_product(
                gathered_copies(model, RCV, 3), columns_all, "fmn,fnc->fmc", False, False
            )
            misfit = traces_f - model.astype(jnp.float32) + complex_scale(wave_re, wave_im, product)
        local_squares = jnp.sum(misfit * misfit, axis=(1, 2, 3))
        misfit_half = misfit.astype(jnp.bfloat16)
        misfit_re = misfit_half[:, 0]
        misfit_im = misfit_half[:, 1]
        column_re = columns_all[:, 0]
        column_im = columns_all[:, 1]
        back_re = paired(misfit_re, column_re) + paired(misfit_im, column_re * 0 + column_im)
        back_im = paired(misfit_im, column_re) - paired(misfit_re, column_im)
        scaled = complex_scale(wave_re, -wave_im, jnp.stack([back_re, back_im], axis=1))
        embedded = lax.dynamic_update_slice(
            jnp.zeros_like(scaled), misfit_half.astype(jnp.float32), (0, 0, 0, col_anchor)
        )
        gradient_rows = lax.psum(embedded - scaled, RCV)
        halfway = complex_product(
            gradient_rows.astype(jnp.bfloat16), forward_cols, "fmn,nc->fmc", False, True
        ).astype(jnp.bfloat16)
        spectrum = column_section(forward_rows, lax.all_gather(halfway, SRC, axis=2, tiled=True))
        trial = coeffs + step_length * spectrum
        magnitude = jnp.sqrt(trial[:, 0] * trial[:, 0] + trial[:, 1] * trial[:, 1])
        local_peak = jnp.max(magnitude, axis=(1, 2))
        global_peak, total_squares = joined_all((local_peak, local_squares), SRC_RCV, combine_stats)
        norm_list.append(jnp.sqrt(total_squares))
        level = shrink_fraction * global_peak[:, None, None]
        factor = jnp.maximum(1.0 - level / jnp.maximum(magnitude, level), 0.0)
        coeffs = trial * factor[:, None]
    return (coeffs, jnp.stack(norm_list))


def solution(mesh):
    split = Mesh(mesh.devices.reshape(4, 4, 4, 2), ("src_0", "src_1", "rcv_0", "rcv_1"))
    return jax.shard_map(
        per_device,
        mesh=split,
        in_specs=(P(None, None, SRC, RCV), P()),
        out_specs=(P(None, None, SRC, RCV), P()),
        check_vma=False,
    )
```

profile of v0, /device:TPU:1, one launch (start us, length us, event | category | flops | bytes accessed | tf_op | source)
XLA Modules:
  0.0 641.2 jit_solution(3735553232752024656)
XLA Ops:
  13.3 51.9 %all-gather.21.cloned.1.call-done = bf16[2,2,2048,256]{3,2,0,1:T(8,128)(2,1)} async-done(((bf16[2,2,128,256]{3,2,0,1:T(8,128)(2,1)}), bf16[2,2,2048,256]{3,2,0,1:T(8,128)(2,1)}) %all-gather.21.cloned.1.call-update) | async-done | bytes 4194320 | tf_op jit(solution)/shard_map/all_gather | solution.py:126
  75.7 56.5 %all-reduce.2 = bf16[2,2,128,2048]{3,2,0,1:T(8,128)(2,1)S(1)} all-reduce(f32[2,2,128,2048]{3,2,0,1:T(8,128)} %maximum_subtract_fusion), channel_id=1, replica_groups=mesh['src_0'=4,'src_1'=4,'rcv_0'=4,'rcv_1'=2] {'rcv_0','rcv_1'}, use_global_device_ids=true, to_apply=%region_0.1 | all-reduce | flops 1048576 | bytes 6291456 | tf_op jit(solution)/shard_map/psum | solution.py:163
  132.2 7.9 %fusion.62 = f32[2,128,256]{2,1,0:T(8,128)S(1)} fusion(s32[256]{0:T(256)S(1)} %iota_add_fusion, bf16[2,2,128,2048]{3,2,0,1:T(8,128)(2,1)S(1)} %all-reduce.2), kind=kOutput, calls=%fused_computation.104 | convolution fusion | flops 276824064 | bytes 1311744 | tf_op jit(solution)/shard_map/fmn,nc->fmc/dot_general | solution.py:91
  140.1 8.1 %fusion.67 = f32[2,128,256]{2,1,0:T(8,128)S(1)} fusion(s32[256]{0:T(256)S(1)} %iota_add_fusion, bf16[2,2,128,2048]{3,2,0,1:T(8,128)(2,1)S(1)} %all-reduce.2), kind=kOutput, calls=%fused_computation.106 | convolution fusion | flops 276824064 | bytes 1311744 | tf_op jit(solution)/shard_map/fmn,nc->fmc/dot_general | solution.py:91
  148.3 8.2 %fusion.44 = bf16[2,1,128,256]{3,2,0,1:T(8,128)(2,1)S(1)} fusion(f32[2,128,256]{2,1,0:T(8,128)S(1)} %fusion.62, s32[256]{0:T(256)S(1)} %iota_add_fusion, bf16[2,2,128,2048]{3,2,0,1:T(8,128)(2,1)S(1)} %all-reduce.2), kind=kOutput, calls=%fused_computation.80 | convolution fusion | flops 276955136 | bytes 1442816 | tf_op jit(solution)/shard_map/fmn,nc->fmc/dot_general | solution.py:91
  156.4 7.9 %fusion.43 = bf16[2,1,128,256]{3,2,0,1:T(8,128)(2,1)S(1)} fusion(f32[2,128,256]{2,1,0:T(8,128)S(1)} %fusion.67, s32[256]{0:T(256)S(1)} %iota_add_fusion, bf16[2,2,128,2048]{3,2,0,1:T(8,128)(2,1)S(1)} %all-reduce.2), kind=kOutput, calls=%fused_computation.79 | convolution fusion | flops 276955136 | bytes 1442816 | tf_op jit(solution)/shard_map/fmn,nc->fmc/dot_general | solution.py:91
  165.5 51.1 %all-gather.23.cloned.1.call-done = bf16[2,2,2048,256]{3,2,0,1:T(8,128)(2,1)} async-done(((bf16[2,2,128,256]{3,2,0,1:T(8,128)(2,1)}), bf16[2,2,2048,256]{3,2,0,1:T(8,128)(2,1)}) %all-gather.23.cloned.1.call-update) | async-done | bytes 4194320 | tf_op jit(solution)/shard_map/all_gather | solution.py:167
  249.6 7.8 %all-gather.10 = f32[4,2,2]{2,1,0:T(2,128)S(1)} all-gather(f32[1,2,2]{2,1,0:T(2,128)S(1)} %maximum_bitcast_fusion.3), channel_id=4, replica_groups=mesh['src_0'=4,'src_1'=4,'rcv_0'=4,'rcv_1'=2] {'rcv_0'}, dimensions={0}, use_global_device_ids=true | all-gather | bytes 80 | tf_op jit(solution)/shard_map/all_gather | solution.py:39
  257.4 8.2 %all-gather.11 = f32[2,2,2]{2,1,0:T(2,128)S(1)} all-gather(f32[1,2,2]{2,1,0:T(2,128)S(1)} %maximum_bitcast_fusion.4), channel_id=5, replica_groups=mesh['src_0'=4,'src_1'=4,'rcv_0'=4,'rcv_1'=2] {'rcv_1'}, dimensions={0}, use_global_device_ids=true | all-gather | bytes 48 | tf_op jit(solution)/shard_map/all_gather | solution.py:39
  267.0 50.0 %all-gather.25.cloned.1.call-done = bf16[2,2,2048,256]{2,3,0,1:T(8,128)(2,1)} async-done(((bf16[2,2,128,256]{2,3,0,1:T(8,128)(2,1)}), bf16[2,2,2048,256]{2,3,0,1:T(8,128)(2,1)}) %all-gather.25.cloned.1.call-update) | async-done | bytes 4194320 | tf_op jit(solution)/shard_map/all_gather | solution.py:142
  336.9 32.3 %all_to_all.10 = bf16[8,2,2,128,256]{4,3,1,2,0:T(8,128)(2,1)S(1)} all-to-all(bf16[8,2,2,128,256]{4,3,1,2,0:T(8,128)(2,1)S(1)} %broadcast_in_dim.4), channel_id=1, replica_groups=mesh['src_0'=4,'src_1'=4,'rcv_0'=4,'rcv_1'=2] {'rcv_0','rcv_1'}, dimensions={0} | all-to-all | bytes 4194304 | tf_op jit(solution)/shard_map/all_to_all | solution.py:24
  369.5 7.9 %fusion.59 = f32[2,128,256]{2,1,0:T(8,128)S(1)} fusion(s32[256]{0:T(256)S(1)} %iota_add_fusion, bf16[2,2,128,2048]{3,2,0,1:T(8,128)(2,1)S(1)} %bitcast.296), kind=kOutput, calls=%fused_computation.103 | convolution fusion | flops 276824064 | bytes 1311744 | tf_op jit(solution)/shard_map/fmn,nc->fmc/dot_general | solution.py:91
  377.4 8.3 %fusion.70 = f32[2,128,256]{2,1,0:T(8,128)S(1)} fusion(s32[256]{0:T(256)S(1)} %iota_add_fusion, bf16[2,2,128,2048]{3,2,0,1:T(8,128)(2,1)S(1)} %bitcast.297), kind=kOutput, calls=%fused_computation.107 | convolution fusion | flops 276824064 | bytes 1311744 | tf_op jit(solution)/shard_map/fmn,nc->fmc/dot_general | solution.py:91
  385.7 8.1 %fusion.42 = bf16[2,1,128,256]{3,2,0,1:T(8,128)(2,1)S(1)} fusion(f32[2,128,256]{2,1,0:T(8,128)S(1)} %fusion.59, s32[256]{0:T(256)S(1)} %iota_add_fusion, bf16[2,2,128,2048]{3,2,0,1:T(8,128)(2,1)S(1)} %bitcast.298), kind=kOutput, calls=%fused_computation.78 | convolution fusion | flops 276955136 | bytes 1442816 | tf_op jit(solution)/shard_map/fmn,nc->fmc/dot_general | solution.py:91
  393.9 7.9 %fusion.41 = bf16[2,1,128,256]{3,2,0,1:T(8,128)(2,1)S(1)} fusion(f32[2,128,256]{2,1,0:T(8,128)S(1)} %fusion.70, s32[256]{0:T(256)S(1)} %iota_add_fusion, bf16[2,2,128,2048]{3,2,0,1:T(8,128)(2,1)S(1)} %bitcast.299), kind=kOutput, calls=%fused_computation.77 | convolution fusion | flops 276955136 | bytes 1442816 | tf_op jit(solution)/shard_map/fmn,nc->fmc/dot_general | solution.py:91
  402.0 29.7 %all_to_all.11 = bf16[8,2,2,128,256]{4,3,1,2,0:T(8,128)(2,1)S(1)} all-to-all(bf16[8,2,2,128,256]{4,3,1,2,0:T(8,128)(2,1)S(1)} %broadcast_in_dim.5), channel_id=1, replica_groups=mesh['src_0'=4,'src_1'=4,'rcv_0'=4,'rcv_1'=2] {'rcv_0','rcv_1'}, dimensions={0} | all-to-all | bytes 4194304 | tf_op jit(solution)/shard_map/all_to_all | solution.py:24
  442.6 56.6 %all-reduce.3 = bf16[2,2,128,2048]{3,2,0,1:T(8,128)(2,1)S(1)} all-reduce(f32[2,2,128,2048]{3,2,0,1:T(8,128)} %maximum_subtract_fusion.1), channel_id=1, replica_groups=mesh['src_0'=4,'src_1'=4,'rcv_0'=4,'rcv_1'=2] {'rcv_0','rcv_1'}, use_global_device_ids=true, to_apply=%region_3.4 | all-reduce | flops 1048576 | bytes 6291456 | tf_op jit(solution)/shard_map/psum | solution.py:163
  499.2 7.9 %fusion.56 = f32[2,128,256]{2,1,0:T(8,128)S(1)} fusion(s32[256]{0:T(256)S(1)} %iota_add_fusion, bf16[2,2,128,2048]{3,2,0,1:T(8,128)(2,1)S(1)} %all-reduce.3), kind=kOutput, calls=%fused_computation.102 | convolution fusion | flops 276824064 | bytes 1311744 | tf_op jit(solution)/shard_map/fmn,nc->fmc/dot_general | solution.py:91
  507.1 8.1 %fusion.64 = f32[2,128,256]{2,1,0:T(8,128)S(1)} fusion(s32[256]{0:T(256)S(1)} %iota_add_fusion, bf16[2,2,128,2048]{3,2,0,1:T(8,128)(2,1)S(1)} %all-reduce.3), kind=kOutput, calls=%fused_computation.105 | convolution fusion | flops 276824064 | bytes 1311744 | tf_op jit(solution)/shard_map/fmn,nc->fmc/dot_general | solution.py:91
  515.2 8.2 %fusion.40 = bf16[2,1,128,256]{3,2,0,1:T(8,128)(2,1)S(1)} fusion(f32[2,128,256]{2,1,0:T(8,128)S(1)} %fusion.56, s32[256]{0:T(256)S(1)} %iota_add_fusion, bf16[2,2,128,2048]{3,2,0,1:T(8,128)(2,1)S(1)} %all-reduce.3), kind=kOutput, calls=%fused_computation.76 | convolution fusion | flops 276955136 | bytes 1442816 | tf_op jit(solution)/shard_map/fmn,nc->fmc/dot_general | solution.py:91
  523.4 7.9 %fusion.39 = bf16[2,1,128,256]{3,2,0,1:T(8,128)(2,1)S(1)} fusion(f32[2,128,256]{2,1,0:T(8,128)S(1)} %fusion.64, s32[256]{0:T(256)S(1)} %iota_add_fusion, bf16[2,2,128,2048]{3,2,0,1:T(8,128)(2,1)S(1)} %all-reduce.3), kind=kOutput, calls=%fused_computation.75 | convolution fusion | flops 276955136 | bytes 1442816 | tf_op jit(solution)/shard_map/fmn,nc->fmc/dot_general | solution.py:91
  532.0 51.3 %all-gather.27.cloned.1.call-done = bf16[2,2,2048,256]{3,2,0,1:T(8,128)(2,1)} async-done(((bf16[2,2,128,256]{3,2,0,1:T(8,128)(2,1)}), bf16[2,2,2048,256]{3,2,0,1:T(8,128)(2,1)}) %all-gather.27.cloned.1.call-update) | async-done | bytes 4194320 | tf_op jit(solution)/shard_map/all_gather | solution.py:167
  616.7 7.8 %all-gather.14 = f32[4,2,2]{2,1,0:T(2,128)S(1)} all-gather(f32[1,2,2]{2,1,0:T(2,128)S(1)} %maximum_bitcast_fusion.7), channel_id=8, replica_groups=mesh['src_0'=4,'src_1'=4,'rcv_0'=4,'rcv_1'=2] {'rcv_0'}, dimensions={0}, use_global_device_ids=true | all-gather | bytes 80 | tf_op jit(solution)/shard_map/all_gather | solution.py:39
  624.5 8.2 %all-gather.15 = f32[2,2,2]{2,1,0:T(2,128)S(1)} all-gather(f32[1,2,2]{2,1,0:T(2,128)S(1)} %maximum_bitcast_fusion.8), channel_id=9, replica_groups=mesh['src_0'=4,'src_1'=4,'rcv_0'=4,'rcv_1'=2] {'rcv_1'}, dimensions={0}, use_global_device_ids=true | all-gather | bytes 48 | tf_op jit(solution)/shard_map/all_gather | solution.py:39
  (94 shorter events, 119.3 us)
Async XLA Ops:
  7.2 58.1 %all-gather.21.cloned.1.call-start = ((), (), s32[]{:S(2)}) async-start(), calls=%async_computation.2 | async-start | bytes 4456448 | tf_op jit(solution)/shard_map/all_gather | solution.py:126
  8.9 207.7 %all-gather.23.cloned.1.call-start = ((), (), s32[]{:S(2)}) async-start(), calls=%async_computation.3 | async-start | bytes 4456448 | tf_op jit(solution)/shard_map/all_gather | solution.py:167
  10.0 2.5 copy-start.2
  65.3 2.8 copy-start
  165.1 151.9 %all-gather.25.cloned.1.call-start = ((), (), s32[]{:S(2)}) async-start(), calls=%async_computation.4 | async-start | bytes 4456448 | tf_op jit(solution)/shard_map/all_gather | solution.py:142
  216.7 6.0 copy-start.3
  266.5 316.8 %all-gather.27.cloned.1.call-start = ((), (), s32[]{:S(2)}) async-start(), calls=%async_computation.5 | async-start | bytes 4456448 | tf_op jit(solution)/shard_map/all_gather | solution.py:167
  317.0 6.1 copy-start.4
  431.7 2.2 copy-start.1
  583.3 6.4 %copy-start.5 = (bf16[2,2,2048,256]{3,2,0,1:T(8,128)(2,1)S(1)}, bf16[2,2,2048,256]{3,2,0,1:T(8,128)(2,1)}, u32[]{:S(2)}) copy-start(bf16[2,2,2048,256]{3,2,0,1:T(8,128)(2,1)} %all-gather.27.cloned.1.call-done) | copy-start | bytes 12582916
Sparse Core Ops, SparseCore 0:
  10.7 54.5 all-gather.20
  165.2 51.4 all-gather.22
  266.6 50.2 all-gather.24
  532.2 51.0 all-gather.26
where the time goes:
time: 645 us; the launch traced here: 641 us
  blocking collectives  234 us (36%)
  waiting for transfers between devices  204 us (32%)
  matrix products  165 us (26%)
  between operations  14.4 us (2%)
  other arithmetic  13.8 us (2%)
  local copies, waits for them, and re-layouts  9 us (1%)
    dot_general x28, matrix products, single(): jnp.einsum(pattern, first_op, second_op, preferred_element_type=jnp.float32)  156 us
    psum x2, blocking collectives, per_device(): gradient_rows = lax.psum(embedded - scaled, RCV)  113 us
    all_gather x2, waiting for transfers between devices, per_device(): lax.all_gather(halfway, SRC, axis=2, tiled=True)  102 us
    all_to_all x2, blocking collectives, copy_for_each(): return lax.all_to_all(copies, axis, split_axis=0, concat_axis=0, tiled=True)  61.9 us
    all_gather x8, blocking collectives, all_in_one(): both, at, found = (lax.all_gather(jnp.concatenate(lines), axis), 0, {})  59 us
    all_gather x1, waiting for transfers between devices, per_device(): columns_all = lax.all_gather(traces, SRC, axis=2, tiled=True)  51.9 us
    all_gather x1, waiting for transfers between devices, per_device(): lax.all_gather(coeff_half, SRC, axis=2, tiled=True)  50 us
  transfers between devices with their start and end apart: 4, of which 4 were waited for; matrix products, arithmetic and copies ran while one was open for 1% of the time, Pallas kernels for 0%

commit v1 on v0

--- a/solution.py
+++ b/solution.py
@@ -139,7 +139,10 @@
         else:
             coeff_half = coeffs.astype(jnp.bfloat16)
             halfway = column_section(
-                inverse_rows, lax.all_gather(coeff_half, SRC, axis=2, tiled=True)
+                inverse_rows,
+                jnp.concatenate(
+                    lax.all_to_all(jnp.stack([coeff_half] * lax.axis_size(SRC)), SRC, 0, 0), axis=2
+                ),
             ).astype(jnp.bfloat16)
             model = complex_product(
                 gathered_copies(halfway, RCV, 3), inverse_cols, "fmn,nc->fmc", False, True

time: 645 us -> 643 us (level)
  waiting for transfers between devices: 204 us -> 152 us
  blocking collectives: 234 us -> 285 us
    all_to_all x0 -> x1, blocking collectives: none -> 53.3 us  [per_device(): lax.all_to_all(jnp.stack([coeff_half] * lax.axis_size(SRC)), SRC, 0, 0)]
    all_gather x1 -> x0, waiting for transfers between devices: 50 us -> none  [per_device(): lax.all_gather(coeff_half, SRC, axis=2, tiled=True)]
  transfers between devices with their start and end apart: 4 -> 3, of which waited for: 4 -> 3; matrix products, arithmetic and copies ran while one was open for 1% -> 1% of each run, Pallas kernels for 0% -> 0%
where the time goes in v1:
time: 643 us; the launch traced here: 639 us
  blocking collectives  285 us (44%)
  matrix products  163 us (25%)
  waiting for transfers between devices  152 us (24%)
  between operations  14.3 us (2%)
  other arithmetic  13.1 us (2%)
  local copies, waits for them, and re-layouts  10.6 us (2%)
    dot_general x28, matrix products, single(): jnp.einsum(pattern, first_op, second_op, preferred_element_type=jnp.float32)  155 us
    psum x2, blocking collectives, per_device(): gradient_rows = lax.psum(embedded - scaled, RCV)  113 us
    all_gather x2, waiting for transfers between devices, per_device(): lax.all_gather(halfway, SRC, axis=2, tiled=True)  100 us
    all_to_all x2, blocking collectives, copy_for_each(): return lax.all_to_all(copies, axis, split_axis=0, concat_axis=0, tiled=True)  59.8 us
    all_gather x8, blocking collectives, all_in_one(): both, at, found = (lax.all_gather(jnp.concatenate(lines), axis), 0, {})  59 us
    all_to_all x1, blocking collectives, per_device(): lax.all_to_all(jnp.stack([coeff_half] * lax.axis_size(SRC)), SRC, 0, 0)  53.3 us
    all_gather x1, waiting for transfers between devices, per_device(): columns_all = lax.all_gather(traces, SRC, axis=2, tiled=True)  51.9 us
  transfers between devices with their start and end apart: 3, of which 3 were waited for; matrix products, arithmetic and copies ran while one was open for 1% of the time, Pallas kernels for 0%

profile of v1, /device:TPU:1, one launch (start us, length us, event | category | flops | bytes accessed | tf_op | source)
XLA Modules:
  0.0 639.0 jit_solution(542015962226861982)
XLA Ops:
  13.3 51.9 %all-gather.20.cloned.1.call-done = bf16[2,2,2048,256]{3,2,0,1:T(8,128)(2,1)} async-done(((bf16[2,2,128,256]{3,2,0,1:T(8,128)(2,1)}), bf16[2,2,2048,256]{3,2,0,1:T(8,128)(2,1)}) %all-gather.20.cloned.1.call-update) | async-done | bytes 4194320 | tf_op jit(solution)/shard_map/all_gather | solution.py:126
  75.7 56.5 %all-reduce.2 = bf16[2,2,128,2048]{3,2,0,1:T(8,128)(2,1)S(1)} all-reduce(f32[2,2,128,2048]{3,2,0,1:T(8,128)} %maximum_subtract_fusion), channel_id=1, replica_groups=mesh['src_0'=4,'src_1'=4,'rcv_0'=4,'rcv_1'=2] {'rcv_0','rcv_1'}, use_global_device_ids=true, to_apply=%region_0.1 | all-reduce | flops 1048576 | bytes 6291456 | tf_op jit(solution)/shard_map/psum | solution.py:166
  132.2 7.9 %fusion.62 = f32[2,128,256]{2,1,0:T(8,128)S(1)} fusion(s32[256]{0:T(256)S(1)} %iota_add_fusion, bf16[2,2,128,2048]{3,2,0,1:T(8,128)(2,1)S(1)} %all-reduce.2), kind=kOutput, calls=%fused_computation.105 | convolution fusion | flops 276824064 | bytes 1311744 | tf_op jit(solution)/shard_map/fmn,nc->fmc/dot_general | solution.py:91
  140.1 8.1 %fusion.67 = f32[2,128,256]{2,1,0:T(8,128)S(1)} fusion(s32[256]{0:T(256)S(1)} %iota_add_fusion, bf16[2,2,128,2048]{3,2,0,1:T(8,128)(2,1)S(1)} %all-reduce.2), kind=kOutput, calls=%fused_computation.107 | convolution fusion | flops 276824064 | bytes 1311744 | tf_op jit(solution)/shard_map/fmn,nc->fmc/dot_general | solution.py:91
  148.2 8.2 %fusion.44 = bf16[2,1,128,256]{3,2,0,1:T(8,128)(2,1)S(1)} fusion(f32[2,128,256]{2,1,0:T(8,128)S(1)} %fusion.62, s32[256]{0:T(256)S(1)} %iota_add_fusion, bf16[2,2,128,2048]{3,2,0,1:T(8,128)(2,1)S(1)} %all-reduce.2), kind=kOutput, calls=%fused_computation.81 | convolution fusion | flops 276955136 | bytes 1442816 | tf_op jit(solution)/shard_map/fmn,nc->fmc/dot_general | solution.py:91
  156.4 7.9 %fusion.43 = bf16[2,1,128,256]{3,2,0,1:T(8,128)(2,1)S(1)} fusion(f32[2,128,256]{2,1,0:T(8,128)S(1)} %fusion.67, s32[256]{0:T(256)S(1)} %iota_add_fusion, bf16[2,2,128,2048]{3,2,0,1:T(8,128)(2,1)S(1)} %all-reduce.2), kind=kOutput, calls=%fused_computation.80 | convolution fusion | flops 276955136 | bytes 1442816 | tf_op jit(solution)/shard_map/fmn,nc->fmc/dot_general | solution.py:91
  165.5 51.1 %all-gather.22.cloned.1.call-done = bf16[2,2,2048,256]{3,2,0,1:T(8,128)(2,1)} async-done(((bf16[2,2,128,256]{3,2,0,1:T(8,128)(2,1)}), bf16[2,2,2048,256]{3,2,0,1:T(8,128)(2,1)}) %all-gather.22.cloned.1.call-update) | async-done | bytes 4194320 | tf_op jit(solution)/shard_map/all_gather | solution.py:170
  249.5 7.8 %all-gather.10 = f32[4,2,2]{2,1,0:T(2,128)S(1)} all-gather(f32[1,2,2]{2,1,0:T(2,128)S(1)} %maximum_bitcast_fusion.3), channel_id=4, replica_groups=mesh['src_0'=4,'src_1'=4,'rcv_0'=4,'rcv_1'=2] {'rcv_0'}, dimensions={0}, use_global_device_ids=true | all-gather | bytes 80 | tf_op jit(solution)/shard_map/all_gather | solution.py:39
  257.4 8.2 %all-gather.11 = f32[2,2,2]{2,1,0:T(2,128)S(1)} all-gather(f32[1,2,2]{2,1,0:T(2,128)S(1)} %maximum_bitcast_fusion.4), channel_id=5, replica_groups=mesh['src_0'=4,'src_1'=4,'rcv_0'=4,'rcv_1'=2] {'rcv_1'}, dimensions={0}, use_global_device_ids=true | all-gather | bytes 48 | tf_op jit(solution)/shard_map/all_gather | solution.py:39
  266.8 53.3 %all_to_all.15 = bf16[16,2,2,128,256]{3,4,1,2,0:T(8,128)(2,1)S(1)} all-to-all(bf16[16,2,2,128,256]{3,4,1,2,0:T(8,128)(2,1)S(1)} %stack.142), channel_id=1, replica_groups=mesh['src_0'=4,'src_1'=4,'rcv_0'=4,'rcv_1'=2] {'src_0','src_1'}, dimensions={0} | all-to-all | bytes 8388608 | tf_op jit(solution)/shard_map/all_to_all | solution.py:144
  338.9 30.1 %all_to_all.16 = bf16[8,2,2,128,256]{4,3,1,2,0:T(8,128)(2,1)S(1)} all-to-all(bf16[8,2,2,128,256]{4,3,1,2,0:T(8,128)(2,1)S(1)} %broadcast_in_dim.4), channel_id=1, replica_groups=mesh['src_0'=4,'src_1'=4,'rcv_0'=4,'rcv_1'=2] {'rcv_0','rcv_1'}, dimensions={0} | all-to-all | bytes 4194304 | tf_op jit(solution)/shard_map/all_to_all | solution.py:24
  369.3 7.9 %fusion.59 = f32[2,128,256]{2,1,0:T(8,128)S(1)} fusion(s32[256]{0:T(256)S(1)} %iota_add_fusion, bf16[2,2,128,2048]{3,2,0,1:T(8,128)(2,1)S(1)} %bitcast.302), kind=kOutput, calls=%fused_computation.104 | convolution fusion | flops 276824064 | bytes 1311744 | tf_op jit(solution)/shard_map/fmn,nc->fmc/dot_general | solution.py:91
  377.2 8.4 %fusion.70 = f32[2,128,256]{2,1,0:T(8,128)S(1)} fusion(s32[256]{0:T(256)S(1)} %iota_add_fusion, bf16[2,2,128,2048]{3,2,0,1:T(8,128)(2,1)S(1)} %bitcast.303), kind=kOutput, calls=%fused_computation.108 | convolution fusion | flops 276824064 | bytes 1311744 | tf_op jit(solution)/shard_map/fmn,nc->fmc/dot_general | solution.py:91
  385.5 8.1 %fusion.42 = bf16[2,1,128,256]{3,2,0,1:T(8,128)(2,1)S(1)} fusion(f32[2,128,256]{2,1,0:T(8,128)S(1)} %fusion.59, s32[256]{0:T(256)S(1)} %iota_add_fusion, bf16[2,2,128,2048]{3,2,0,1:T(8,128)(2,1)S(1)} %bitcast.304), kind=kOutput, calls=%fused_computation.79 | convolution fusion | flops 276955136 | bytes 1442816 | tf_op jit(solution)/shard_map/fmn,nc->fmc/dot_general | solution.py:91
  393.7 7.9 %fusion.41 = bf16[2,1,128,256]{3,2,0,1:T(8,128)(2,1)S(1)} fusion(f32[2,128,256]{2,1,0:T(8,128)S(1)} %fusion.70, s32[256]{0:T(256)S(1)} %iota_add_fusion, bf16[2,2,128,2048]{3,2,0,1:T(8,128)(2,1)S(1)} %bitcast.305), kind=kOutput, calls=%fused_computation.78 | convolution fusion | flops 276955136 | bytes 1442816 | tf_op jit(solution)/shard_map/fmn,nc->fmc/dot_general | solution.py:91
  401.8 29.7 %all_to_all.17 = bf16[8,2,2,128,256]{4,3,1,2,0:T(8,128)(2,1)S(1)} all-to-all(bf16[8,2,2,128,256]{4,3,1,2,0:T(8,128)(2,1)S(1)} %broadcast_in_dim.5), channel_id=1, replica_groups=mesh['src_0'=4,'src_1'=4,'rcv_0'=4,'rcv_1'=2] {'rcv_0','rcv_1'}, dimensions={0} | all-to-all | bytes 4194304 | tf_op jit(solution)/shard_map/all_to_all | solution.py:24
  442.5 56.6 %all-reduce.3 = bf16[2,2,128,2048]{3,2,0,1:T(8,128)(2,1)S(1)} all-reduce(f32[2,2,128,2048]{3,2,0,1:T(8,128)} %maximum_subtract_fusion.1), channel_id=1, replica_groups=mesh['src_0'=4,'src_1'=4,'rcv_0'=4,'rcv_1'=2] {'rcv_0','rcv_1'}, use_global_device_ids=true, to_apply=%region_3.4 | all-reduce | flops 1048576 | bytes 6291456 | tf_op jit(solution)/shard_map/psum | solution.py:166
  499.0 7.9 %fusion.56 = f32[2,128,256]{2,1,0:T(8,128)S(1)} fusion(s32[256]{0:T(256)S(1)} %iota_add_fusion, bf16[2,2,128,2048]{3,2,0,1:T(8,128)(2,1)S(1)} %all-reduce.3), kind=kOutput, calls=%fused_computation.103 | convolution fusion | flops 276824064 | bytes 1311744 | tf_op jit(solution)/shard_map/fmn,nc->fmc/dot_general | solution.py:91
  506.9 8.1 %fusion.64 = f32[2,128,256]{2,1,0:T(8,128)S(1)} fusion(s32[256]{0:T(256)S(1)} %iota_add_fusion, bf16[2,2,128,2048]{3,2,0,1:T(8,128)(2,1)S(1)} %all-reduce.3), kind=kOutput, calls=%fused_computation.106 | convolution fusion | flops 276824064 | bytes 1311744 | tf_op jit(solution)/shard_map/fmn,nc->fmc/dot_general | solution.py:91
  515.0 8.2 %fusion.40 = bf16[2,1,128,256]{3,2,0,1:T(8,128)(2,1)S(1)} fusion(f32[2,128,256]{2,1,0:T(8,128)S(1)} %fusion.56, s32[256]{0:T(256)S(1)} %iota_add_fusion, bf16[2,2,128,2048]{3,2,0,1:T(8,128)(2,1)S(1)} %all-reduce.3), kind=kOutput, calls=%fused_computation.77 | convolution fusion | flops 276955136 | bytes 1442816 | tf_op jit(solution)/shard_map/fmn,nc->fmc/dot_general | solution.py:91
  523.2 7.9 %fusion.39 = bf16[2,1,128,256]{3,2,0,1:T(8,128)(2,1)S(1)} fusion(f32[2,128,256]{2,1,0:T(8,128)S(1)} %fusion.64, s32[256]{0:T(256)S(1)} %iota_add_fusion, bf16[2,2,128,2048]{3,2,0,1:T(8,128)(2,1)S(1)} %all-reduce.3), kind=kOutput, calls=%fused_computation.76 | convolution fusion | flops 276955136 | bytes 1442816 | tf_op jit(solution)/shard_map/fmn,nc->fmc/dot_general | solution.py:91
  531.9 49.2 %all-gather.24.cloned.1.call-done = bf16[2,2,2048,256]{3,2,0,1:T(8,128)(2,1)} async-done(((bf16[2,2,128,256]{3,2,0,1:T(8,128)(2,1)}), bf16[2,2,2048,256]{3,2,0,1:T(8,128)(2,1)}) %all-gather.24.cloned.1.call-update) | async-done | bytes 4194320 | tf_op jit(solution)/shard_map/all_gather | solution.py:170
  614.4 7.8 %all-gather.14 = f32[4,2,2]{2,1,0:T(2,128)S(1)} all-gather(f32[1,2,2]{2,1,0:T(2,128)S(1)} %maximum_bitcast_fusion.7), channel_id=8, replica_groups=mesh['src_0'=4,'src_1'=4,'rcv_0'=4,'rcv_1'=2] {'rcv_0'}, dimensions={0}, use_global_device_ids=true | all-gather | bytes 80 | tf_op jit(solution)/shard_map/all_gather | solution.py:39
  622.3 8.2 %all-gather.15 = f32[2,2,2]{2,1,0:T(2,128)S(1)} all-gather(f32[1,2,2]{2,1,0:T(2,128)S(1)} %maximum_bitcast_fusion.8), channel_id=9, replica_groups=mesh['src_0'=4,'src_1'=4,'rcv_0'=4,'rcv_1'=2] {'rcv_1'}, dimensions={0}, use_global_device_ids=true | all-gather | bytes 48 | tf_op jit(solution)/shard_map/all_gather | solution.py:39
  (92 shorter events, 118.0 us)
Async XLA Ops:
  7.2 58.1 %all-gather.20.cloned.1.call-start = ((), (), s32[]{:S(2)}) async-start(), calls=%async_computation.3 | async-start | bytes 4456448 | tf_op jit(solution)/shard_map/all_gather | solution.py:126
  8.9 207.7 %all-gather.22.cloned.1.call-start = ((), (), s32[]{:S(2)}) async-start(), calls=%async_computation.4 | async-start | bytes 4456448 | tf_op jit(solution)/shard_map/all_gather | solution.py:170
  10.0 2.5 copy-start.2
  65.3 2.8 copy-start
  165.1 416.0 %all-gather.24.cloned.1.call-start = ((), (), s32[]{:S(2)}) async-start(), calls=%async_computation.5 | async-start | bytes 4456448 | tf_op jit(solution)/shard_map/all_gather | solution.py:170
  216.6 6.0 copy-start.3
  431.5 2.2 copy-start.1
  581.1 6.4 %copy-start.4 = (bf16[2,2,2048,256]{3,2,0,1:T(8,128)(2,1)S(1)}, bf16[2,2,2048,256]{3,2,0,1:T(8,128)(2,1)}, u32[]{:S(2)}) copy-start(bf16[2,2,2048,256]{3,2,0,1:T(8,128)(2,1)} %all-gather.24.cloned.1.call-done) | copy-start | bytes 12582916
Sparse Core Ops, SparseCore 0:
  10.7 54.5 all-gather.19
  165.2 51.4 all-gather.21
  532.0 49.0 all-gather.23
